TPU v7x, 8 devices: a whole 2x2x1 slice. The times are simulated.
8 devices in a mesh: data: 2 (over z, y), expert: 4 (over x, core).
Axes of the slice: x: 2, y: 2, z: 1, core: 2. Of those that a mesh axis runs over, the one named last changes fastest.
Arguments:
- x_tok: bfloat16 [16384, 2304], P(('data', 'expert')), parts along dimension 0
- topk_idx: int32 [16384, 2], P(('data', 'expert')), parts along dimension 0
- topk_w: float32 [16384, 2], P(('data', 'expert')), parts along dimension 0
- w_up: bfloat16 [8, 2304, 5760], P('expert')
- w_down: bfloat16 [8, 5760, 2304], P('expert')
Outputs:
- output: bfloat16 [16384, 2304], P(('data', 'expert')), parts along dimension 0
There are 2 independent parts. A program takes and returns all parts, laid end to end along the dimension named above; an argument that names none is the same for every part.
All inputs are finite; a program needn't handle non-finite values.
Results may differ from a plain program's by a relative error of at most 0.001.
Values are sent between devices in bfloat16 or wider.
A program may use at most 1 GiB of HBM per device.

v0:
```python
import jax
import jax.numpy as jnp
from jax import lax
from jax.sharding import PartitionSpec as P, NamedSharding


def route_slots(idx_loc, n_exp, slot_cap):
    top_k = idx_loc.shape[1]
    pair_exp = idx_loc.reshape(-1)
    n_pairs = pair_exp.shape[0]
    sort_order = jnp.argsort(pair_exp, stable=True)
    pair_rank = jnp.argsort(sort_order, stable=True)
    counts = jnp.bincount(pair_exp, length=n_exp)
    starts = jnp.cumsum(counts) - counts
    slot_src = jnp.minimum(starts[:, None] + jnp.arange(slot_cap)[None, :], n_pairs - 1)
    slot_tok = (sort_order[slot_src] // top_k).reshape(-1)
    pair_slot = pair_exp * slot_cap + pair_rank - starts[pair_exp]
    return slot_tok, pair_slot


def solution(mesh):
    group_size = mesh.shape['expert']

    def local_moe(x_loc, idx_loc, gate_loc, up_loc, down_loc):
        tok_dev, d_model = x_loc.shape
        top_k = idx_loc.shape[1]
        exp_local = up_loc.shape[0]
        n_exp = exp_local * group_size
        slot_cap = min(4, n_exp // top_k) * tok_dev * top_k // n_exp
        slot_tok, pair_slot = route_slots(idx_loc, n_exp, slot_cap)
        send_rows = jnp.take(x_loc, slot_tok, axis=0).reshape(group_size, exp_local, slot_cap, d_model)
        recv_rows = lax.all_to_all(send_rows, 'expert', 0, 0, tiled=True)
        hidden = jnp.einsum('secm,emf->secf', recv_rows, up_loc, preferred_element_type=jnp.float32)
        hidden = jax.nn.gelu(hidden, approximate=True).astype(jnp.bfloat16)
        expert_out = jnp.einsum('secf,efm->secm', hidden, down_loc, preferred_element_type=jnp.float32).astype(jnp.bfloat16)
        back_rows = lax.all_to_all(expert_out, 'expert', 0, 0, tiled=True).reshape(n_exp * slot_cap, d_model)
        pair_out = jnp.take(back_rows, pair_slot, axis=0).reshape(tok_dev, top_k, d_model)
        combined = jnp.sum(gate_loc[:, :, None] * pair_out.astype(jnp.float32), axis=1)
        return combined.astype(jnp.bfloat16)

    tok_spec = P(('data', 'expert'), None)
    w_spec = P('expert', None, None)
    return jax.shard_map(local_moe, mesh=mesh, in_specs=(tok_spec, tok_spec, tok_spec, w_spec, w_spec), out_specs=tok_spec, check_vma=False)
```

profile of v0, /device:TPU:0, one launch (start us, length us, event | category | flops | bytes accessed | tf_op | source)
XLA Modules:
  0.0 3322.0 jit_solution(8312774272005915890)
XLA Ops:
  0.0 1.1 copy.14
  1.1 0.6 reshape.223
  1.7 0.0 copy-start.2
  1.7 0.5 reshape.222
  2.2 28.8 scatter_custom_fusion
  31.0 0.2 reduce-window.9
  31.2 0.6 copy-done.7
  31.8 0.1 fusion.12
  31.9 5.8 sort.31
  37.7 90.5 %gather_fusion = s32[16384]{0:T(1024)S(1)} fusion(s32[4096]{0:T(1024)S(1)} %get-tuple-element.7, s32[16384]{0:T(1024)S(1)} %broadcast_clamp_fusion.1), kind=kCustom, calls=%fused_computation | custom fusion | bytes 196608 | tf_op jit(solution)/shard_map/gather | solution.py:16
  128.3 0.3 compare_select_fusion
  128.7 0.8 compare_and_fusion
  129.5 141.3 %gather_fusion.1 = bf16[16384,2304]{1,0:T(8,128)(2,1)} fusion(bf16[2048,2304]{1,0:T(8,128)(2,1)} %param.5, s32[16384]{0:T(1024)S(1)} %broadcast_clamp_fusion), kind=kCustom, calls=%fused_computation.1 | custom fusion | bytes 151060480 | tf_op jit(solution)/shard_map/jit(_take)/gather | solution.py:31
  270.8 0.0 copy-done.2
  270.9 50.0 %broadcast_select_fusion = bf16[4,2,2048,2304]{3,2,1,0:T(8,128)(2,1)} fusion(bf16[4,2,2048,2304]{3,2,1,0:T(8,128)(2,1)} %bitcast.14, pred[4,2,2048]{2,1,0:T(4,128)(4,1)S(1)} %copy-done.6), kind=kLoop, calls=%fused_computation.15 | loop fusion | flops 37748736 | bytes 151011328 | tf_op jit(solution)/shard_map/jit(_take)/select_n | solution.py:31
  320.9 849.0 %all_to_all.10 = bf16[4,2,2048,2304]{3,2,1,0:T(8,128)(2,1)} all-to-all(bf16[4,2,2048,2304]{3,2,1,0:T(8,128)(2,1)} %broadcast_select_fusion), channel_id=1, replica_groups=mesh['data'=2,'expert'=4] {'expert'}, dimensions={0} | all-to-all | bytes 150994944 | tf_op jit(solution)/shard_map/all_to_all | solution.py:32
  1169.9 554.6 %fusion.7 = bf16[4,2,2048,5760]{3,2,0,1:T(8,128)(2,1)} fusion(bf16[4,2,2048,2304]{3,2,1,0:T(8,128)(2,1)} %all_to_all.10, bf16[2,2304,5760]{2,1,0:T(8,128)(2,1)} %param.8), kind=kOutput, calls=%fused_computation.12 | convolution fusion | flops 435714785280 | bytes 317325312 | tf_op jit(solution)/shard_map/secm,emf->secf/dot_general | solution.py:33
  1724.5 491.0 %fusion.9 = bf16[4,2,2048,2304]{3,2,0,1:T(8,128)(2,1)} fusion(bf16[4,2,2048,5760]{3,2,0,1:T(8,128)(2,1)} %fusion.7, bf16[2,5760,2304]{2,1,0:T(8,128)(2,1)} %param.9), kind=kOutput, calls=%fused_computation.16 | convolution fusion | flops 434903187456 | bytes 317325312 | tf_op jit(solution)/shard_map/secf,efm->secm/dot_general | solution.py:35
  2215.6 50.1 %copy.17 = bf16[4,2,2048,2304]{3,2,1,0:T(8,128)(2,1)} copy(bf16[4,2,2048,2304]{3,2,0,1:T(8,128)(2,1)} %fusion.9) | data formatting | bytes 150994944 | tf_op jit(solution)/shard_map/convert_element_type | solution.py:35
  2265.7 0.0 copy-start.9
  2265.7 14.7 all-to-all-start.1
  2280.5 5.8 sort.32
  2286.3 0.7 fusion.15
  2287.0 0.1 compare_reduce_fusion
  2287.0 4.5 compare_select_fusion.7
  2291.6 0.7 compare_and_fusion.1
  2292.2 1.1 broadcast_in_dim.34
  2293.4 0.4 copy.13
  2293.8 798.6 %all-to-all-done.1 = bf16[4,2,2048,2304]{3,2,1,0:T(8,128)(2,1)} async-done(((bf16[4,2,2048,2304]{3,2,1,0:T(8,128)(2,1)}), bf16[4,2,2048,2304]{3,2,1,0:T(8,128)(2,1)}, u32[]{:S(2)}, u32[]{:S(2)}) %all-to-all-start.1) | async-done | bytes 75497504 | tf_op jit(solution)/shard_map/all_to_all | solution.py:36
  3092.4 100.6 %gather_fusion.2 = bf16[4096,2304]{1,0:T(8,128)(2,1)} fusion(bf16[16384,2304]{1,0:T(8,128)(2,1)} %bitcast.21, s32[4096]{0:T(1024)S(1)} %broadcast_clamp_fusion.2), kind=kCustom, calls=%fused_computation.2 | custom fusion | bytes 37765120 | tf_op jit(solution)/shard_map/jit(_take)/gather | solution.py:37
  3193.0 36.4 %gather.29 = bf16[2048,2,2304]{2,1,0:T(2,128)(2,1)} reshape(bf16[4096,2304]{1,0:T(8,128)(2,1)} %gather_fusion.2) | data formatting | bytes 37748736 | tf_op jit(solution)/shard_map/jit(_take)/gather | solution.py:37
  3229.3 92.7 %multiply_reduce_fusion = bf16[2048,2304]{1,0:T(8,128)(2,1)} fusion(bf16[2048,2,2304]{2,1,0:T(2,128)(2,1)} %gather.29, pred[2048,2]{1,0:T(8,128)(4,1)S(1)} %broadcast_in_dim.34, f32[2048,2]{1,0:T(8,128)S(1)} %copy.13), kind=kLoop, calls=%fused_computation.19 | loop fusion | flops 33030144 | bytes 28332032 | tf_op jit(solution)/shard_map/reduce_sum | solution.py:38
  (26 shorter events, 0.1 us)
Async XLA Ops:
  1.7 269.1 %copy-start.2 = (s32[4096,1]{0,1:T(1,128)}, s32[4096,1]{0,1:T(1,128)S(1)}, u32[]{:S(2)}) copy-start(s32[4096,1]{0,1:T(1,128)S(1)} %reshape.223) | copy-start | bytes 49156
  2.2 268.6 %copy-start.4 = (s32[4096]{0:T(1024)}, s32[4096]{0:T(1024)S(1)}, u32[]{:S(2)}) copy-start(s32[4096]{0:T(1024)S(1)} %reshape.222) | copy-start | bytes 49156
  31.2 0.6 copy-start.7
  37.7 233.1 %copy-start = (s32[4096]{0:T(1024)}, s32[4096]{0:T(1024)S(1)}, u32[]{:S(2)}) copy-start(s32[4096]{0:T(1024)S(1)} %get-tuple-element.7) | copy-start | bytes 49156
  129.5 141.3 %copy-start.6 = (pred[4,2,2048]{2,1,0:T(4,128)(4,1)S(1)}, pred[4,2,2048]{2,1,0:T(4,128)(4,1)}, u32[]{:S(2)}) copy-start(pred[4,2,2048]{2,1,0:T(4,128)(4,1)} %compare_and_fusion) | copy-start | bytes 49156
  2265.7 14.8 copy-start.1
  2265.7 20.6 copy-start.8
  2265.7 21.3 copy-start.3
  2265.7 25.9 copy-start.5
  2265.7 27.7 copy-start.9
  2265.7 826.6 %all-to-all-start.1 = ((bf16[4,2,2048,2304]{3,2,1,0:T(8,128)(2,1)}), bf16[4,2,2048,2304]{3,2,1,0:T(8,128)(2,1)}, u32[]{:S(2)}, u32[]{:S(2)}) async-start(bf16[4,2,2048,2304]{3,2,1,0:T(8,128)(2,1)} %copy.17), calls=%async_computation.1 | async-start | bytes 150994944 | tf_op jit(solution)/shard_map/all_to_all | solution.py:36
where the time goes:
time: 3330 us; the launch traced here: 3320 us
  matrix products  1050 us (32%)
  blocking collectives  849 us (25%)
  waiting for transfers between devices  799 us (24%)
  local copies, waits for them, and re-layouts  424 us (13%)
  other arithmetic  190 us (6%)
    all_to_all x1, blocking collectives, local_moe(): recv_rows = lax.all_to_all(send_rows, 'expert', 0, 0, tiled=True)  849 us
    all_to_all x1, waiting for transfers between devices, local_moe(): lax.all_to_all(expert_out, 'expert', 0, 0, tiled=True)  799 us
    dot_general x1, matrix products, local_moe(): jnp.einsum('secm,emf->secf', recv_rows, up_loc, preferred_element_type=jn...  555 us
    dot_general x1, matrix products, local_moe(): jnp.einsum('secf,efm->secm', hidden, down_loc, preferred_element_type=jnp...  491 us
    gather x1, local copies, waits for them, and re-layouts, local_moe(): jnp.take(x_loc, slot_tok, axis=0)  141 us
    gather x2, local copies, waits for them, and re-layouts, local_moe(): jnp.take(back_rows, pair_slot, axis=0).reshape(tok_dev, top_k, d_model)  137 us
    reduce_sum x1, other arithmetic, local_moe(): jnp.sum(gate_loc[:, :, None] * pair_out.astype(jnp.float32), axis=1)  92.7 us
    gather x2, local copies, waits for them, and re-layouts, route_slots(): slot_tok = (sort_order[slot_src] // top_k).reshape(-1)  90.6 us
  transfers between devices with their start and end apart: 1, of which 1 were waited for; matrix products, arithmetic and copies ran while one was open for 0% of the time, Pallas kernels for 0%

commit v1 on v0

v1 whole, which is shorter than its diff:
```python
import functools

import jax
import jax.numpy as jnp
from jax import lax
from jax.experimental import pallas as pl
from jax.experimental.pallas import tpu as pltpu
from jax.sharding import PartitionSpec as P


F32, BF16, I32 = jnp.float32, jnp.bfloat16, jnp.int32
HOT_ROWS = 1024
COLD_ROWS = 1024
STEP = 128
GATHER = STEP
UP_COLS = 1920
DOWN_COLS = 768
VMEM_LIMIT = 60 << 20
ANY = pl.BlockSpec(memory_space=pl.ANY)


def params(n):
    return pltpu.CompilerParams(dimension_semantics=("arbitrary",) * n, vmem_limit_bytes=VMEM_LIMIT)


def gelu(v):
    return jax.nn.gelu(v, approximate=True).astype(BF16)


def prep_body(cap, scal, idx_ref, base_ref, pos_ref, cnt_ref):
    hot, own, r1, r2 = scal[0], scal[1], scal[2], scal[3]
    w = 256
    tri = (lax.broadcasted_iota(I32, (w, w), 0) <= lax.broadcasted_iota(I32, (w, w), 1)).astype(F32)
    base = ((base_ref[...] + STEP - 1) // STEP * STEP)[:, 0:1].astype(F32)
    carry = jnp.zeros((8, 1), F32)
    pos_ref[...] = jnp.full(pos_ref.shape, -1, I32)
    for b in range(idx_ref.shape[1] // w):
        cols = pl.ds(b * w, w)
        c0, c1 = idx_ref[0:1, cols], idx_ref[1:2, cols]
        cold = jnp.where(c0 == hot, c1, c0)
        loc = jnp.where(cold == own, 0, jnp.where(cold == own + 1, 1, jnp.where(cold == r1, 2, jnp.where(cold == r2, 3, -1))))
        mine = (lax.broadcasted_iota(I32, (8, w), 0) == loc).astype(F32)
        upto = jnp.dot(mine, tri, preferred_element_type=F32) + carry
        rank = jnp.sum(mine * (upto + base - 1.0), axis=0, keepdims=True).astype(I32)
        pos_ref[0:1, cols] = jnp.where(loc >= 0, loc * cap + rank, -1)
        carry = upto[:, w - 1:w]
    cnt_ref[...] = jnp.broadcast_to(carry, (8, 128)).astype(I32)


def prep(scal, idx8, base, cap):
    vmem = pl.BlockSpec(memory_space=pltpu.VMEM)
    return pl.pallas_call(
        functools.partial(prep_body, cap),
        out_shape=(jax.ShapeDtypeStruct(idx8.shape, I32), jax.ShapeDtypeStruct((8, 128), I32)),
        in_specs=[pl.BlockSpec(memory_space=pltpu.SMEM), vmem, vmem],
        out_specs=(vmem, vmem),
    )(scal, idx8, base)


def gather_body(n_parts, blk, pos_ref, *refs):
    parts, out_ref = refs[:n_parts], refs[-1]
    i = pl.program_id(0)

    @pl.when(i < blk[pl.num_programs(0)])
    def _():
        total, start = None, 0
        for part in parts:
            width = part.shape[0]
            slot = blk[i] * GATHER + lax.broadcasted_iota(I32, (GATHER, width), 0)
            pick = (pos_ref[0:1, start:start + width] == slot).astype(F32).astype(BF16)
            term = jnp.dot(pick, part[...], preferred_element_type=F32)
            total = term if total is None else total + term
            start += width
        out_ref[...] = total.astype(BF16)


def gather(blk, pos, parts, slots, prev, dep):
    d = parts[0].shape[1]
    alias = prev is not None
    return pl.pallas_call(
        functools.partial(gather_body, len(parts)),
        out_shape=jax.ShapeDtypeStruct((slots, d), BF16),
        grid_spec=pltpu.PrefetchScalarGridSpec(
            num_scalar_prefetch=1, grid=(blk.shape[0] - 1,),
            in_specs=[pl.BlockSpec(pos.shape, lambda i, b: (0, 0))]
            + [pl.BlockSpec(p.shape, lambda i, b: (0, 0)) for p in parts] + [ANY] * (1 + alias),
            out_specs=pl.BlockSpec((GATHER, d), lambda i, b: (b[i], 0))),
        input_output_aliases={3 + len(parts): 0} if alias else {},
        compiler_params=params(1),
    )(blk, pos, *parts, dep, *([prev] if alias else []))


def ffn_body(n_sets, rb, hot, x_ref, *refs):
    metas, ups, downs = refs[:n_sets], refs[n_sets:2 * n_sets], refs[2 * n_sets:3 * n_sets]
    out_ref, hid_ref = refs[-2:]
    d, ff = ups[0].shape[1:]

    def for_rows(meta, i, run):
        if hot:
            lax.fori_loop(0, rb // 512, lambda r, c: (run(r * 512, 512), c)[1], 0)
            return
        steps = meta[2, i]
        lax.fori_loop(0, steps // 2, lambda r, c: (run(r * 256, 256), c)[1], 0)

        @pl.when(steps % 2 == 1)
        def _():
            run((steps - 1) * STEP, STEP)

    for meta, up, down in zip(metas, ups, downs):
        n = meta[3, 0]

        def up_step(step, x, w, h, meta=meta):
            def run(r, m):
                rows = pl.ds(pl.multiple_of(r, m), m)
                h[rows, :] = gelu(jnp.dot(x[rows, :], w[0], preferred_element_type=F32))

            for_rows(meta, step.index[0], run)

        def down_step(step, h, w, o, meta=meta):
            if not hot:
                o[...] = jnp.zeros_like(o)

            def run(r, m):
                rows = pl.ds(pl.multiple_of(r, m), m)
                o[rows, :] = jnp.dot(h[rows, :], w[0], preferred_element_type=F32).astype(BF16)

            for_rows(meta, step.index[0], run)

        @pl.when(n > 0)
        def _(meta=meta, up=up, down=down, up_step=up_step, down_step=down_step, n=n):
            pltpu.emit_pipeline(
                up_step, grid=(n, ff // UP_COLS),
                in_specs=[pl.BlockSpec((rb, d), lambda i, f: (meta[0, i], 0)),
                          pl.BlockSpec((1, d, UP_COLS), lambda i, f: (meta[1, i], 0, f))],
                out_specs=[pl.BlockSpec((rb, UP_COLS), lambda i, f: (i, f))],
                _explicit_indices=True,
            )(x_ref, up, hid_ref)
            pltpu.emit_pipeline(
                down_step, grid=(n, d // DOWN_COLS),
                in_specs=[pl.BlockSpec((rb, ff), lambda i, c: (i, 0)),
                          pl.BlockSpec((1, ff, DOWN_COLS), lambda i, c: (meta[1, i], 0, c))],
                out_specs=[pl.BlockSpec((rb, DOWN_COLS), lambda i, c: (meta[0, i], c))],
                _explicit_indices=True,
            )(hid_ref, down, out_ref)


def ffn(sets, x, dep, prev, rb, hot, out_rows):
    n = len(sets)
    metas, ups, downs = zip(*sets)
    d, ff = ups[0].shape[1:]
    max_items = max(m.shape[1] for m in metas)
    alias = prev is not None
    out, _ = pl.pallas_call(
        functools.partial(ffn_body, n, rb, hot),
        out_shape=(jax.ShapeDtypeStruct((out_rows, d), BF16), jax.ShapeDtypeStruct((max_items * rb, ff), BF16)),
        in_specs=[ANY] + [pl.BlockSpec(memory_space=pltpu.SMEM)] * n + [ANY] * (2 * n + 1 + alias),
        out_specs=(ANY, ANY),
        input_output_aliases={3 * n + 2: 0} if alias else {},
        compiler_params=pltpu.CompilerParams(vmem_limit_bytes=VMEM_LIMIT),
    )(x, *metas, *ups, *downs, dep, *([prev] if alias else []))
    return out


def after_body(value, dep, out):
    out[0] = value[0]


def after(value, dep):
    smem = pl.BlockSpec(memory_space=pltpu.SMEM)
    return pl.pallas_call(after_body, out_shape=jax.ShapeDtypeStruct((1,), I32), in_specs=[smem, ANY], out_specs=smem)(
        value.astype(I32)[None], dep)[0]


def join_body(local, blk, scal, pos_ref, gate_ref, hot_ref, cold_ref, out_ref, acc):
    k = pl.program_id(1)
    t = pos_ref.shape[0]

    @pl.when(k == 0)
    def _():
        acc[...] = jnp.zeros_like(acc)

    @pl.when(k < blk[pl.num_programs(1)])
    def _():
        slot = blk[k] * GATHER + lax.broadcasted_iota(I32, (t, GATHER), 1)
        pick = (pos_ref[:, 0:1] == slot).astype(F32).astype(BF16)
        acc[...] += jnp.dot(pick, cold_ref[...], preferred_element_type=F32)

    @pl.when(k == pl.num_programs(1) - 1)
    def _():
        for r in range(0, t, 256):
            rows = slice(r, r + 256)
            here = jnp.broadcast_to(pos_ref[rows, 0:1], (256, acc.shape[1])) >= 0
            g_hot, g_cold = gate_ref[rows, 0:1], gate_ref[rows, 1:2]
            o_hot, o_cold = hot_ref[rows, :].astype(F32), acc[rows, :]

            @pl.when(scal[0] == 1)
            def _():
                if local:
                    out_ref[rows, :] = g_hot * o_hot + jnp.where(here, g_cold * o_cold, 0.0)
                else:
                    out_ref[rows, :] = jnp.where(here, g_hot * o_hot + g_cold * o_cold, o_hot).astype(BF16)

            @pl.when(scal[0] == 0)
            def _():
                if local:
                    out_ref[rows, :] = jnp.where(here, g_cold * o_cold, 0.0)
                else:
                    out_ref[rows, :] = o_cold.astype(BF16)


def join(blk, scal, pos_col, gates, o_hot, o_cold, local, first, rows):
    d = o_hot.shape[1]
    tb = 1024
    return pl.pallas_call(
        functools.partial(join_body, local),
        out_shape=jax.ShapeDtypeStruct((rows, d), F32 if local else BF16),
        grid_spec=pltpu.PrefetchScalarGridSpec(
            num_scalar_prefetch=2, grid=(rows // tb, blk.shape[0] - 1),
            in_specs=[pl.BlockSpec((tb, 1), lambda i, k, b, s: (i + first, 0)),
                      pl.BlockSpec((tb, 2), lambda i, k, b, s: (i + first, 0)),
                      pl.BlockSpec((tb, d), lambda i, k, b, s: (i, 0)),
                      pl.BlockSpec((GATHER, d), lambda i, k, b, s: (b[k], 0))],
            out_specs=pl.BlockSpec((tb, d), lambda i, k, b, s: (i, 0)),
            scratch_shapes=[pltpu.VMEM((tb, d), F32)]),
        compiler_params=params(2),
    )(blk, scal, pos_col, gates, o_hot, o_cold)


def final_body(part_ref, gate_ref, back_ref, prev_ref, out_ref):
    out_ref[...] = (part_ref[...] + gate_ref[...] * back_ref[...].astype(F32)).astype(BF16)


def final(part, gate, back, prev, half):
    rows, d = part.shape
    tb = 256
    n = rows // 2 // tb
    return pl.pallas_call(
        final_body,
        out_shape=jax.ShapeDtypeStruct((rows, d), BF16),
        grid=(n,),
        in_specs=[pl.BlockSpec((tb, d), lambda i: (i + half * n, 0)), pl.BlockSpec((tb, 1), lambda i: (i + half * n, 0)),
                  pl.BlockSpec((tb, d), lambda i: (i, 0)), ANY],
        out_specs=pl.BlockSpec((tb, d), lambda i: (i + half * n, 0)),
        input_output_aliases={3: 0} if prev is not None else {},
        compiler_params=params(1),
    )(part, gate, back, prev if prev is not None else back)


def cold_items(steps, locs, cap):
    per = COLD_ROWS // STEP
    n = [(steps[l] + per - 1) // per for l in locs]
    i = jnp.arange(cap // COLD_ROWS + len(locs), dtype=I32)
    block, exp, left = locs[0] * (cap // COLD_ROWS) + i, jnp.zeros_like(i), steps[locs[0]] - i * per
    if len(locs) == 2:
        second = i >= n[0]
        j = i - n[0]
        block = jnp.where(second, locs[1] * (cap // COLD_ROWS) + j, block)
        exp = second.astype(I32)
        left = jnp.where(second, steps[locs[1]] - j * per, left)
    return jnp.stack([jnp.clip(block, 0, 4 * cap // COLD_ROWS - 1), exp, jnp.clip(left, 1, per), jnp.full_like(i, sum(n))])


def gather_blocks(n, first, cap, tokens):
    i = jnp.arange(tokens // GATHER + 4, dtype=I32)
    i = jnp.minimum(i, sum(n) - 1)
    blk, start = jnp.zeros_like(i), 0
    for l in range(4):
        blk = jnp.where(i >= start, l * (cap // GATHER) + first[l] + i - start, blk)
        start = start + n[l]
    return jnp.concatenate([jnp.clip(blk, 0, 4 * cap // GATHER - 1), jnp.full((1,), start, I32)])


def solution(mesh):
    group = mesh.shape['expert']
    n_exp = 2 * group
    sib = [(i, i ^ 1) for i in range(group)]
    far = [(i, i ^ 2) for i in range(group)]

    def send(v, pairs):
        return lax.ppermute(v, 'expert', pairs)

    def layer(x, idx, gate, up, down):
        tokens, _ = x.shape
        half = tokens // 2
        cap = 2 * tokens
        me = lax.axis_index('expert')
        p_idx = send(idx, far)
        p_gate = send(gate, far)

        taken = [jnp.sum((idx == k).astype(I32)) == tokens for k in range(n_exp)]
        hot = sum(jnp.where(t, k, 0) for k, t in enumerate(taken)).astype(I32)
        owner = hot // 2
        sel = jnp.where(owner == me, hot % 2, 0)
        peer = me ^ 1
        p_sel = jnp.where(owner == peer, hot % 2, 0)
        ids = jnp.stack([hot, 2 * me, 2 * peer + p_sel, 2 * peer + 1 - p_sel]).astype(I32)
        hot_here = owner // 2 == me // 2
        flag = hot_here.astype(I32)[None]

        far1 = send(x[:half], far)
        far2 = send(x[half:], far)
        sel_1 = after(sel, idx)
        up1 = lax.dynamic_slice_in_dim(up, sel_1, 1, 0)
        down1 = lax.dynamic_slice_in_dim(down, after(sel_1, up1), 1, 0)
        other = after(1 - sel_1, down1)
        up1 = send(up1, sib)
        down1 = send(down1, sib)

        def rows8(i):
            return jnp.concatenate([i.T, jnp.full((6, tokens), -1, I32)], axis=0)

        pos_o, cnt_o = prep(ids, rows8(idx), jnp.zeros((8, 128), I32), cap)
        pos_p, cnt_p = prep(ids, rows8(p_idx), cnt_o, cap)
        n_o = [(cnt_o[l, 0] + STEP - 1) // STEP for l in range(4)]
        n_p = [(cnt_p[l, 0] + STEP - 1) // STEP for l in range(4)]
        n_all = [a + b for a, b in zip(n_o, n_p)]
        blk_o = gather_blocks(n_o, [0] * 4, cap, tokens)
        blk_p = gather_blocks(n_p, n_o, cap, tokens)
        col_o, col_p = pos_o[0][:, None], pos_p[0][:, None]

        rows_o = gather(blk_o, pos_o, (x,), 4 * cap, None, pos_o)
        up2 = send(lax.dynamic_slice_in_dim(up, other, 1, 0), sib)
        down2 = send(lax.dynamic_slice_in_dim(down, other, 1, 0), sib)

        def gates(i, g):
            first = i[:, 0:1] == hot
            return jnp.concatenate([jnp.where(first, g[:, 0:1], g[:, 1:2]), jnp.where(first, g[:, 1:2], g[:, 0:1])], axis=1)

        g_o, g_p = gates(idx, gate), gates(p_idx, p_gate)
        here = col_o >= 0
        g_back = jnp.where(hot_here, jnp.where(here, 0.0, g_o[:, 1:2]), jnp.where(here, g_o[:, 0:1], 1.0))
        own_hot, got_hot = (owner == me).astype(I32), (owner == peer).astype(I32)

        def run_hot(xs, first, n, sets, dep, prev):
            i = jnp.arange(n, dtype=I32)
            sets = [(jnp.stack([i + first, jnp.full_like(i, exp), i, jnp.full_like(i, n * on)]), u, dn) for exp, on, u, dn in sets]
            return ffn(sets, xs, dep, prev, HOT_ROWS, True, xs.shape[0])

        hot_own, hot_got = (hot % 2, own_hot, up, down), (0, got_hot, up1, down1)
        hot_o = run_hot(x, 0, 2, [hot_own], rows_o, None)
        hot_1 = run_hot(far1, 0, 1, [hot_own, hot_got], hot_o, None)
        hot_o = run_hot(x, 0, 1, [hot_got], hot_1, hot_o)
        rows = gather(blk_p, pos_p, (far1, far2), 4 * cap, rows_o, hot_o)
        sets = [(cold_items(n_all, (0, 1), cap), up, down), (cold_items(n_all, (2,), cap), up1, down1),
                (cold_items(n_all, (3,), cap), up2, down2)]
        cold = ffn(sets, rows, rows, None, COLD_ROWS, False, 4 * cap)
        out_1 = join(blk_p, flag, col_p, g_p, hot_1, cold, False, 0, half)
        back_1 = send(out_1, far)
        hot_2 = run_hot(far2, 0, 1, [hot_own, hot_got], out_1, None)
        out_2 = join(blk_p, flag, col_p, g_p, hot_2, cold, False, 1, half)
        back_2 = send(out_2, far)
        hot_o = run_hot(x, 1, 1, [hot_got], out_2, hot_o)
        part = join(blk_o, flag, col_o, g_o, hot_o, cold, True, 0, tokens)
        y = final(part, g_back, back_1, None, 0)
        return final(part, g_back, back_2, y, 1)

    tok_spec = P(('data', 'expert'), None)
    w_spec = P('expert', None, None)
    return jax.shard_map(layer, mesh=mesh, in_specs=(tok_spec, tok_spec, tok_spec, w_spec, w_spec), out_specs=tok_spec, check_vma=False)
```

time: 3330 us -> 891 us (0.27)
  the two profiles are of different devices: /device:TPU:0 before, /device:TPU:1 now
where the time goes in v1:
time: 891 us; the launch traced here: 883 us
  Pallas kernels  445 us (50%)
  starting transfers between devices  176 us (20%)
  waiting for transfers between devices  135 us (15%)
  local copies, waits for them, and re-layouts  101 us (11%)
  between operations  15.9 us (2%)
  other arithmetic  10.2 us (1%)
    pallas_call x6, Pallas kernels, ffn(): pl.pallas_call(functools.partial(ffn_body, n, rb, hot), out_shape=(jax.Sh...  277 us
    ppermute x10, starting transfers between devices, send(): return lax.ppermute(v, 'expert', pairs)  176 us
    ppermute x10, waiting for transfers between devices, send(): return lax.ppermute(v, 'expert', pairs)  135 us
    pallas_call x3, Pallas kernels, join(): pl.pallas_call(functools.partial(join_body, local), out_shape=jax.ShapeDt...  101 us
    pallas_call x2, Pallas kernels, gather(): pl.pallas_call(functools.partial(gather_body, len(parts)), out_shape=jax....  45.2 us
    dynamic_slice x1, local copies, waits for them, and re-layouts, layer(): up1 = lax.dynamic_slice_in_dim(up, sel_1, 1, 0)  21.3 us
    dynamic_slice x1, local copies, waits for them, and re-layouts, layer(): up2 = send(lax.dynamic_slice_in_dim(up, other, 1, 0), sib)  21.2 us
    dynamic_slice x1, local copies, waits for them, and re-layouts, layer(): down2 = send(lax.dynamic_slice_in_dim(down, other, 1, 0), sib)  18.5 us
  transfers between devices with their start and end apart: 10, of which 3 were waited for; matrix products, arithmetic and copies ran while one was open for 10% of the time, Pallas kernels for 19%

profile of v1, /device:TPU:1, one launch (start us, length us, event | category | flops | bytes accessed | tf_op | source)
XLA Modules:
  0.0 883.3 jit_solution(8288008557586101946)
XLA Ops:
  0.0 1.6 fusion.6
  6.0 2.1 copy.99.dep
  10.2 21.3 %constant_dynamic-slice_fusion.3.dep = bf16[1,2304,5760]{2,1,0:T(8,128)(2,1)} fusion(bf16[2,2304,5760]{2,1,0:T(8,128)(2,1)} %refs_2_.5, s32[]{:T(128)S(6)} %select_n.195), kind=kLoop, calls=%fused_computation.40 | loop fusion | bytes 53084164 | tf_op jit(solution)/shard_map/dynamic_slice | solution.py:303
  34.5 18.4 %constant_dynamic-slice_fusion.2.dep = bf16[1,5760,2304]{2,1,0:T(8,128)(2,1)} fusion(bf16[2,5760,2304]{2,1,0:T(8,128)(2,1)} %refs_4_.3, s32[]{:T(128)S(6)} %select_n.196), kind=kLoop, calls=%fused_computation.39 | loop fusion | bytes 53084164 | tf_op jit(solution)/shard_map/dynamic_slice | solution.py:304
  56.2 21.2 %constant_dynamic-slice_fusion.1 = bf16[1,2304,5760]{2,1,0:T(8,128)(2,1)} fusion(bf16[2,2304,5760]{2,1,0:T(8,128)(2,1)} %refs_2_.5, s32[]{:T(128)S(6)} %select_n.213), kind=kLoop, calls=%fused_computation.38 | loop fusion | bytes 53084164 | tf_op jit(solution)/shard_map/dynamic_slice | solution.py:322
  77.5 18.5 %constant_dynamic-slice_fusion = bf16[1,5760,2304]{2,1,0:T(8,128)(2,1)} fusion(bf16[2,5760,2304]{2,1,0:T(8,128)(2,1)} %refs_4_.3, s32[]{:T(128)S(6)} %select_n.213), kind=kLoop, calls=%fused_computation.37 | loop fusion | bytes 53084164 | tf_op jit(solution)/shard_map/dynamic_slice | solution.py:323
  96.4 2.2 collective-permute-start.2
  99.8 1.5 collective-permute-start.3
  101.2 6.5 fusion.18
  107.8 101.6 %collective-permute-done.5.x_ref.refs_0_ = bf16[1024,2304]{1,0:T(8,128)(2,1)} collective-permute-done((bf16[1024,2304]{1,0:T(8,128)(2,1)S(1)}, bf16[1024,2304]{1,0:T(8,128)(2,1)}, u32[]{:S(2)}, u32[]{:S(2)}) %collective-permute-start.5) | collective-permute-done | bytes 4718624 | tf_op jit(solution)/shard_map/ppermute | solution.py:280
  211.5 2.1 shard_map.55
  213.7 1.4 fusion.23
  221.2 2.1 shard_map.58
  223.4 1.4 fusion.22
  228.5 1.4 copy.112.pos_ref
  231.7 23.9 %shard_map.59.refs_3_ = bf16[16384,2304]{1,0:T(8,128)(2,1)} custom-call(s32[21]{0:T(128)} %pad_add_fusion.5.blk, s32[8,2048]{1,0:T(8,128)} %get-tuple-element.16.pos_ref.refs_1_, bf16[2048,2304]{1,0:T(8,128)(2,1)} %x_ref.5, s32[8,2048]{1,0:T(8,128)} %get-tuple-element.16.pos_ref.refs_1_), custom_call_target="tpu_custom_call" | custom-call | tf_op jit(solution)/shard_map/pallas_call | solution.py:80
  255.6 8.8 shard_map.60
  266.5 1.3 pad_maximum_fusion.1.gate_ref
  267.8 9.3 %shard_map.61 = (bf16[1024,2304]{1,0:T(8,128)(2,1)}, bf16[1024,5760]{1,0:T(8,128)(2,1)}) custom-call(bf16[1024,2304]{1,0:T(8,128)(2,1)} %collective-permute-done.5.x_ref.refs_0_, s32[4,1]{1,0:T(4,128)} %copy.110.refs_0_, s32[4,1]{1,0:T(4,128)} %copy.111.refs_1_.refs_0_, bf16[2,2304,5760]{2,1,0:T(8,128)(2,1)} %refs_2_.5, ...), custom_call_target="tpu_custom_call" | custom-call | tf_op jit(solution)/shard_map/pallas_call | solution.py:153
  277.8 32.4 %collective-permute-done.4.refs_1_.x_ref = bf16[1024,2304]{1,0:T(8,128)(2,1)} collective-permute-done((bf16[1024,2304]{1,0:T(8,128)(2,1)}, bf16[1024,2304]{1,0:T(8,128)(2,1)}, u32[]{:S(2)}, u32[]{:S(2)}) %collective-permute-start.4) | collective-permute-done | bytes 4718624 | tf_op jit(solution)/shard_map/ppermute | solution.py:280
  310.2 21.3 %shard_map.63.x_ref.refs_9_ = bf16[16384,2304]{1,0:T(8,128)(2,1)} custom-call(s32[21]{0:T(128)} %pad_add_fusion.6.blk, s32[8,2048]{1,0:T(8,128)} %get-tuple-element.18.pos_ref, bf16[1024,2304]{1,0:T(8,128)(2,1)} %collective-permute-done.5.x_ref.refs_0_, bf16[1024,2304]{1,0:T(8,128)(2,1)} %collective-permute-done.4.refs_1_.x_ref, ...), custom_call_target="tpu_custom_call", output_to_operand_aliasing={{}: (5, {})} | custom-call | tf_op jit(solution)/shard_map/pallas_call | solution.py:80
  331.6 241.3 %shard_map.65 = (bf16[16384,2304]{1,0:T(8,128)(2,1)}, bf16[6144,5760]{1,0:T(8,128)(2,1)}) custom-call(bf16[16384,2304]{1,0:T(8,128)(2,1)} %shard_map.63.x_ref.refs_9_, s32[4,6]{1,0:T(4,128)} %add_add_fusion.1.refs_0_, s32[4,5]{1,0:T(4,128)} %get-tuple-element.52.refs_1_, s32[4,5]{1,0:T(4,128)} %get-tuple-element.51.refs_2_, bf16[2,2304,5760]{2,1,0:T(8,128)(2,1)} %refs_2_.5, ...), custom_call_target="tpu_custom_call" | custom-call | tf_op jit(solution)/shard_map/pallas_call | solution.py:153
  572.9 23.9 %shard_map.66.refs_6_ = bf16[1024,2304]{1,0:T(8,128)(2,1)} custom-call(s32[21]{0:T(128)} %pad_add_fusion.6.blk, s32[1]{0:T(128)} %bitcast.10.scal, s32[2048,1]{1,0:T(8,128)} %copy.112.pos_ref, f32[2048,2]{1,0:T(8,128)} %pad_maximum_fusion.1.gate_ref, bf16[1024,2304]{1,0:T(8,128)(2,1)} %get-tuple-element.20.refs_3_.hot_ref, ...), custom_call_target="tpu_custom_call" | custom-call | tf_op jit(solution)/shard_map/pallas_call | solution.py:214
  596.7 100.5 %collective-permute-start.9 = (bf16[1024,2304]{1,0:T(8,128)(2,1)}, bf16[1024,2304]{1,0:T(8,128)(2,1)}, u32[]{:S(2)}, u32[]{:S(2)}) collective-permute-start(bf16[1024,2304]{1,0:T(8,128)(2,1)} %shard_map.66.refs_6_), channel_id=1, source_target_pairs={{0,2},{1,3},{2,0},{3,1},{4,6},{5,7},{6,4},{7,5}} | collective-permute-start | bytes 14155784 | tf_op jit(solution)/shard_map/ppermute | solution.py:280
  697.2 15.8 %shard_map.67 = (bf16[1024,2304]{1,0:T(8,128)(2,1)}, bf16[1024,5760]{1,0:T(8,128)(2,1)}) custom-call(bf16[1024,2304]{1,0:T(8,128)(2,1)} %collective-permute-done.4.refs_1_.x_ref, s32[4,1]{1,0:T(4,128)} %copy.110.refs_0_, s32[4,1]{1,0:T(4,128)} %copy.111.refs_1_.refs_0_, bf16[2,2304,5760]{2,1,0:T(8,128)(2,1)} %refs_2_.5, ...), custom_call_target="tpu_custom_call" | custom-call | tf_op jit(solution)/shard_map/pallas_call | solution.py:153
  713.1 24.2 %shard_map.68.refs_3_ = bf16[1024,2304]{1,0:T(8,128)(2,1)} custom-call(s32[21]{0:T(128)} %pad_add_fusion.6.blk, s32[1]{0:T(128)} %bitcast.10.scal, s32[2048,1]{1,0:T(8,128)} %copy.112.pos_ref, f32[2048,2]{1,0:T(8,128)} %pad_maximum_fusion.1.gate_ref, bf16[1024,2304]{1,0:T(8,128)(2,1)} %get-tuple-element.23.hot_ref, ...), custom_call_target="tpu_custom_call" | custom-call | tf_op jit(solution)/shard_map/pallas_call | solution.py:214
  737.2 70.6 %collective-permute-start.8 = (bf16[1024,2304]{1,0:T(8,128)(2,1)}, bf16[1024,2304]{1,0:T(8,128)(2,1)}, u32[]{:S(2)}, u32[]{:S(2)}) collective-permute-start(bf16[1024,2304]{1,0:T(8,128)(2,1)} %shard_map.68.refs_3_), channel_id=1, source_target_pairs={{0,2},{1,3},{2,0},{3,1},{4,6},{5,7},{6,4},{7,5}} | collective-permute-start | bytes 14155784 | tf_op jit(solution)/shard_map/ppermute | solution.py:280
  811.0 1.3 select_select_fusion
  812.2 1.3 pad_maximum_fusion.gate_ref
  814.4 53.2 %shard_map.70.part_ref = f32[2048,2304]{1,0:T(8,128)} custom-call(s32[21]{0:T(128)} %pad_add_fusion.5.blk, s32[1]{0:T(128)} %bitcast.10.scal, s32[2048,1]{1,0:T(8,128)} %copy-done, f32[2048,2]{1,0:T(8,128)} %pad_maximum_fusion.gate_ref, bf16[2048,2304]{1,0:T(8,128)(2,1)} %get-tuple-element.24.hot_ref, bf16[16384,2304]{1,0:T(8,128)(2,1)} %get-tuple-element.22.cold_ref), custom_call_target="tpu_custom_call" | custom-call | tf_op jit(solution)/shard_map/pallas_call | solution.py:214
  867.7 7.7 shard_map.71.prev_ref
  875.4 7.7 shard_map.72
  (72 shorter events, 19.7 us)
Async XLA Ops:
  31.5 236.3 %collective-permute-start = (bf16[1,2304,5760]{2,1,0:T(8,128)(2,1)}, bf16[1,2304,5760]{2,1,0:T(8,128)(2,1)}, u32[]{:S(2)}, u32[]{:S(2)}) collective-permute-start(bf16[1,2304,5760]{2,1,0:T(8,128)(2,1)} %constant_dynamic-slice_fusion.3.dep), channel_id=1, source_target_pairs={{0,1},{1,0},{2,3},{3,2},{4,5},{5,4},{6,7},{7,6}} | collective-permute-start | bytes 79626248 | tf_op jit(solution)/shard_map/ppermute | solution.py:280
  53.0 214.8 %collective-permute-start.1 = (bf16[1,5760,2304]{2,1,0:T(8,128)(2,1)}, bf16[1,5760,2304]{2,1,0:T(8,128)(2,1)}, u32[]{:S(2)}, u32[]{:S(2)}) collective-permute-start(bf16[1,5760,2304]{2,1,0:T(8,128)(2,1)} %constant_dynamic-slice_fusion.2.dep), channel_id=1, source_target_pairs={{0,1},{1,0},{2,3},{3,2},{4,5},{5,4},{6,7},{7,6}} | collective-permute-start | bytes 79626248 | tf_op jit(solution)/shard_map/ppermute | solution.py:280
  77.5 18.9 %copy-start.1 = (s32[2048,2]{0,1:T(2,128)S(1)}, s32[2048,2]{0,1:T(2,128)}, u32[]{:S(2)}) copy-start(s32[2048,2]{0,1:T(2,128)} %param.6) | copy-start | bytes 49156
  77.5 22.3 %copy-start.3 = (f32[2048,2]{0,1:T(2,128)S(1)}, f32[2048,2]{0,1:T(2,128)}, u32[]{:S(2)}) copy-start(f32[2048,2]{0,1:T(2,128)} %param.7) | copy-start | bytes 49156
  77.5 254.1 %collective-permute-start.6 = (bf16[1,2304,5760]{2,1,0:T(8,128)(2,1)}, bf16[1,2304,5760]{2,1,0:T(8,128)(2,1)}, u32[]{:S(2)}, u32[]{:S(2)}) collective-permute-start(bf16[1,2304,5760]{2,1,0:T(8,128)(2,1)} %constant_dynamic-slice_fusion.1), channel_id=1, source_target_pairs={{0,1},{1,0},{2,3},{3,2},{4,5},{5,4},{6,7},{7,6}} | collective-permute-start | bytes 79626248 | tf_op jit(solution)/shard_map/ppermute | solution.py:280
  95.9 235.6 %collective-permute-start.7 = (bf16[1,5760,2304]{2,1,0:T(8,128)(2,1)}, bf16[1,5760,2304]{2,1,0:T(8,128)(2,1)}, u32[]{:S(2)}, u32[]{:S(2)}) collective-permute-start(bf16[1,5760,2304]{2,1,0:T(8,128)(2,1)} %constant_dynamic-slice_fusion), channel_id=1, source_target_pairs={{0,1},{1,0},{2,3},{3,2},{4,5},{5,4},{6,7},{7,6}} | collective-permute-start | bytes 79626248 | tf_op jit(solution)/shard_map/ppermute | solution.py:280
  96.4 3.4 collective-permute-start.2
  99.8 8.0 collective-permute-start.3
  107.8 101.6 %collective-permute-start.5 = (bf16[1024,2304]{1,0:T(8,128)(2,1)S(1)}, bf16[1024,2304]{1,0:T(8,128)(2,1)}, u32[]{:S(2)}, u32[]{:S(2)}) collective-permute-start(bf16[1024,2304]{1,0:T(8,128)(2,1)S(1)} %get-tuple-element.35), channel_id=1, source_target_pairs={{0,2},{1,3},{2,0},{3,1},{4,6},{5,7},{6,4},{7,5}} | collective-permute-start | bytes 14155784 | tf_op jit(solution)/shard_map/ppermute | solution.py:280
  209.3 100.9 %collective-permute-start.4 = (bf16[1024,2304]{1,0:T(8,128)(2,1)}, bf16[1024,2304]{1,0:T(8,128)(2,1)}, u32[]{:S(2)}, u32[]{:S(2)}) collective-permute-start(bf16[1024,2304]{1,0:T(8,128)(2,1)} %get-tuple-element.36), channel_id=1, source_target_pairs={{0,2},{1,3},{2,0},{3,1},{4,6},{5,7},{6,4},{7,5}} | collective-permute-start | bytes 14155784 | tf_op jit(solution)/shard_map/ppermute | solution.py:280
  596.7 270.9 %collective-permute-start.9 = (bf16[1024,2304]{1,0:T(8,128)(2,1)}, bf16[1024,2304]{1,0:T(8,128)(2,1)}, u32[]{:S(2)}, u32[]{:S(2)}) collective-permute-start(bf16[1024,2304]{1,0:T(8,128)(2,1)} %shard_map.66.refs_6_), channel_id=1, source_target_pairs={{0,2},{1,3},{2,0},{3,1},{4,6},{5,7},{6,4},{7,5}} | collective-permute-start | bytes 14155784 | tf_op jit(solution)/shard_map/ppermute | solution.py:280
  713.0 94.8 %copy-start.5 = (s32[4,1]{0,1:T(1,128)S(1)}, s32[4,1]{0,1:T(1,128)}, u32[]{:S(2)}) copy-start(s32[4,1]{0,1:T(1,128)} %get-tuple-element.54) | copy-start | bytes 52
  713.0 96.6 %copy-start.2 = (s32[2048,2]{0,1:T(2,128)S(1)}, s32[2048,2]{0,1:T(2,128)}, u32[]{:S(2)}) copy-start(s32[2048,2]{0,1:T(2,128)} %param.6) | copy-start | bytes 49156
  713.1 97.1 %copy-start.4 = (f32[2048,2]{0,1:T(2,128)S(1)}, f32[2048,2]{0,1:T(2,128)}, u32[]{:S(2)}) copy-start(f32[2048,2]{0,1:T(2,128)} %param.7) | copy-start | bytes 49156
  737.2 138.2 %collective-permute-start.8 = (bf16[1024,2304]{1,0:T(8,128)(2,1)}, bf16[1024,2304]{1,0:T(8,128)(2,1)}, u32[]{:S(2)}, u32[]{:S(2)}) collective-permute-start(bf16[1024,2304]{1,0:T(8,128)(2,1)} %shard_map.68.refs_3_), channel_id=1, source_target_pairs={{0,2},{1,3},{2,0},{3,1},{4,6},{5,7},{6,4},{7,5}} | collective-permute-start | bytes 14155784 | tf_op jit(solution)/shard_map/ppermute | solution.py:280
  809.7 4.8 copy-start

commit v2 on v1

--- a/solution.py
+++ b/solution.py
@@ -100,7 +100,11 @@
             lax.fori_loop(0, rb // 512, lambda r, c: (run(r * 512, 512), c)[1], 0)
             return
         steps = meta[2, i]
-        lax.fori_loop(0, steps // 2, lambda r, c: (run(r * 256, 256), c)[1], 0)
+        lax.fori_loop(0, steps // 4, lambda r, c: (run(r * 512, 512), c)[1], 0)
+
+        @pl.when(steps % 4 >= 2)
+        def _():
+            run(steps // 4 * 512, 256)
 
         @pl.when(steps % 2 == 1)
         def _():

time: 891 us -> 897 us (level)
  the two profiles are of different devices: /device:TPU:1 before, /device:TPU:2 now
where the time goes in v2:
time: 897 us; the launch traced here: 890 us
  Pallas kernels  653 us (73%)
  waiting for transfers between devices  104 us (12%)
  local copies, waits for them, and re-layouts  101 us (11%)
  between operations  16.2 us (2%)
  other arithmetic  10.2 us (1%)
    pallas_call x6, Pallas kernels, ffn(): pl.pallas_call(functools.partial(ffn_body, n, rb, hot), out_shape=(jax.Sh...  508 us
    ppermute x10, waiting for transfers between devices, send(): return lax.ppermute(v, 'expert', pairs)  104 us
    pallas_call x3, Pallas kernels, join(): pl.pallas_call(functools.partial(join_body, local), out_shape=jax.ShapeDt...  87.2 us
    pallas_call x2, Pallas kernels, gather(): pl.pallas_call(functools.partial(gather_body, len(parts)), out_shape=jax....  35.5 us
    dynamic_slice x1, local copies, waits for them, and re-layouts, layer(): up1 = lax.dynamic_slice_in_dim(up, sel_1, 1, 0)  21.3 us
    dynamic_slice x1, local copies, waits for them, and re-layouts, layer(): up2 = send(lax.dynamic_slice_in_dim(up, other, 1, 0), sib)  21.2 us
    dynamic_slice x1, local copies, waits for them, and re-layouts, layer(): down2 = send(lax.dynamic_slice_in_dim(down, other, 1, 0), sib)  18.5 us
    dynamic_slice x1, local copies, waits for them, and re-layouts, layer(): down1 = lax.dynamic_slice_in_dim(down, after(sel_1, up1), 1, 0)  18.4 us
  transfers between devices with their start and end apart: 10, of which 2 were waited for; matrix products, arithmetic and copies ran while one was open for 10% of the time, Pallas kernels for 50%

profile of v2, /device:TPU:2, one launch (start us, length us, event | category | flops | bytes accessed | tf_op | source)
XLA Modules:
  0.0 889.5 jit_solution(3755480174889226606)
XLA Ops:
  0.0 1.6 fusion.6
  6.0 2.1 copy.99.dep
  10.2 21.3 %constant_dynamic-slice_fusion.3.dep = bf16[1,2304,5760]{2,1,0:T(8,128)(2,1)} fusion(bf16[2,2304,5760]{2,1,0:T(8,128)(2,1)} %refs_2_.5, s32[]{:T(128)S(6)} %select_n.195), kind=kLoop, calls=%fused_computation.40 | loop fusion | bytes 53084164 | tf_op jit(solution)/shard_map/dynamic_slice | solution.py:307
  34.5 18.4 %constant_dynamic-slice_fusion.2.dep = bf16[1,5760,2304]{2,1,0:T(8,128)(2,1)} fusion(bf16[2,5760,2304]{2,1,0:T(8,128)(2,1)} %refs_4_.3, s32[]{:T(128)S(6)} %select_n.196), kind=kLoop, calls=%fused_computation.39 | loop fusion | bytes 53084164 | tf_op jit(solution)/shard_map/dynamic_slice | solution.py:308
  56.2 21.2 %constant_dynamic-slice_fusion.1 = bf16[1,2304,5760]{2,1,0:T(8,128)(2,1)} fusion(bf16[2,2304,5760]{2,1,0:T(8,128)(2,1)} %refs_2_.5, s32[]{:T(128)S(6)} %select_n.213), kind=kLoop, calls=%fused_computation.38 | loop fusion | bytes 53084164 | tf_op jit(solution)/shard_map/dynamic_slice | solution.py:326
  77.5 18.5 %constant_dynamic-slice_fusion = bf16[1,5760,2304]{2,1,0:T(8,128)(2,1)} fusion(bf16[2,5760,2304]{2,1,0:T(8,128)(2,1)} %refs_4_.3, s32[]{:T(128)S(6)} %select_n.213), kind=kLoop, calls=%fused_computation.37 | loop fusion | bytes 53084164 | tf_op jit(solution)/shard_map/dynamic_slice | solution.py:327
  96.4 3.7 collective-permute-done.2
  100.2 6.5 fusion.18
  106.7 2.0 collective-permute-start.5
  108.7 100.7 %collective-permute-done.5.x_ref.refs_0_ = bf16[1024,2304]{1,0:T(8,128)(2,1)} collective-permute-done((bf16[1024,2304]{1,0:T(8,128)(2,1)S(1)}, bf16[1024,2304]{1,0:T(8,128)(2,1)}, u32[]{:S(2)}, u32[]{:S(2)}) %collective-permute-start.5) | collective-permute-done | bytes 4718624 | tf_op jit(solution)/shard_map/ppermute | solution.py:284
  209.4 1.7 collective-permute-start.4
  213.0 2.1 shard_map.55
  215.2 1.4 fusion.23
  222.7 2.1 shard_map.58
  224.9 1.4 fusion.22
  230.0 1.4 copy.112.pos_ref
  233.3 16.9 %shard_map.59.refs_3_ = bf16[16384,2304]{1,0:T(8,128)(2,1)} custom-call(s32[21]{0:T(128)} %pad_add_fusion.5.blk, s32[8,2048]{1,0:T(8,128)} %get-tuple-element.16.pos_ref.refs_1_, bf16[2048,2304]{1,0:T(8,128)(2,1)} %x_ref.5, s32[8,2048]{1,0:T(8,128)} %get-tuple-element.16.pos_ref.refs_1_), custom_call_target="tpu_custom_call" | custom-call | tf_op jit(solution)/shard_map/pallas_call | solution.py:80
  250.2 8.9 %shard_map.60 = (bf16[2048,2304]{1,0:T(8,128)(2,1)}, bf16[2048,5760]{1,0:T(8,128)(2,1)}) custom-call(bf16[2048,2304]{1,0:T(8,128)(2,1)} %x_ref.5, s32[4,2]{1,0:T(4,128)} %add_add_fusion.refs_0_, bf16[2,2304,5760]{2,1,0:T(8,128)(2,1)} %refs_2_.5, bf16[2,5760,2304]{2,1,0:T(8,128)(2,1)} %refs_4_.3, bf16[16384,2304]{1,0:T(8,128)(2,1)} %shard_map.59.refs_3_), custom_call_target="tpu_custom_call" | custom-call | tf_op jit(solution)/shard_map/pallas_call | solution.py:157
  261.2 1.3 pad_maximum_fusion.1.gate_ref
  262.5 78.7 %shard_map.61 = (bf16[1024,2304]{1,0:T(8,128)(2,1)}, bf16[1024,5760]{1,0:T(8,128)(2,1)}) custom-call(bf16[1024,2304]{1,0:T(8,128)(2,1)} %collective-permute-done.5.x_ref.refs_0_, s32[4,1]{1,0:T(4,128)} %copy.110.refs_0_, s32[4,1]{1,0:T(4,128)} %copy.111.refs_1_.refs_0_, bf16[2,2304,5760]{2,1,0:T(8,128)(2,1)} %refs_2_.5, ...), custom_call_target="tpu_custom_call" | custom-call | tf_op jit(solution)/shard_map/pallas_call | solution.py:157
  341.3 78.5 %shard_map.62 = (bf16[2048,2304]{1,0:T(8,128)(2,1)}, bf16[1024,5760]{1,0:T(8,128)(2,1)}) custom-call(bf16[2048,2304]{1,0:T(8,128)(2,1)} %x_ref.5, s32[4,1]{1,0:T(4,128)} %copy.111.refs_1_.refs_0_, bf16[1,2304,5760]{2,1,0:T(8,128)(2,1)} %collective-permute-done.refs_3_.refs_1_.refs_4_, ...), custom_call_target="tpu_custom_call", output_to_operand_aliasing={{0}: (5, {})} | custom-call | tf_op jit(solution)/shard_map/pallas_call | solution.py:157
  419.7 18.6 %shard_map.63.x_ref.refs_9_ = bf16[16384,2304]{1,0:T(8,128)(2,1)} custom-call(s32[21]{0:T(128)} %pad_add_fusion.6.blk, s32[8,2048]{1,0:T(8,128)} %get-tuple-element.18.pos_ref, bf16[1024,2304]{1,0:T(8,128)(2,1)} %collective-permute-done.5.x_ref.refs_0_, bf16[1024,2304]{1,0:T(8,128)(2,1)} %collective-permute-done.4.refs_1_.x_ref, ...), custom_call_target="tpu_custom_call", output_to_operand_aliasing={{}: (5, {})} | custom-call | tf_op jit(solution)/shard_map/pallas_call | solution.py:80
  438.3 179.7 %shard_map.65 = (bf16[16384,2304]{1,0:T(8,128)(2,1)}, bf16[6144,5760]{1,0:T(8,128)(2,1)}) custom-call(bf16[16384,2304]{1,0:T(8,128)(2,1)} %shard_map.63.x_ref.refs_9_, s32[4,6]{1,0:T(4,128)} %add_add_fusion.1.refs_0_, s32[4,5]{1,0:T(4,128)} %get-tuple-element.52.refs_1_, s32[4,5]{1,0:T(4,128)} %get-tuple-element.51.refs_2_, bf16[2,2304,5760]{2,1,0:T(8,128)(2,1)} %refs_2_.5, ...), custom_call_target="tpu_custom_call" | custom-call | tf_op jit(solution)/shard_map/pallas_call | solution.py:157
  618.0 23.1 %shard_map.66.refs_6_ = bf16[1024,2304]{1,0:T(8,128)(2,1)} custom-call(s32[21]{0:T(128)} %pad_add_fusion.6.blk, s32[1]{0:T(128)} %bitcast.10.scal, s32[2048,1]{1,0:T(8,128)} %copy.112.pos_ref, f32[2048,2]{1,0:T(8,128)} %pad_maximum_fusion.1.gate_ref, bf16[1024,2304]{1,0:T(8,128)(2,1)} %get-tuple-element.20.refs_3_.hot_ref, ...), custom_call_target="tpu_custom_call" | custom-call | tf_op jit(solution)/shard_map/pallas_call | solution.py:218
  641.1 83.9 %shard_map.67 = (bf16[1024,2304]{1,0:T(8,128)(2,1)}, bf16[1024,5760]{1,0:T(8,128)(2,1)}) custom-call(bf16[1024,2304]{1,0:T(8,128)(2,1)} %collective-permute-done.4.refs_1_.x_ref, s32[4,1]{1,0:T(4,128)} %copy.110.refs_0_, s32[4,1]{1,0:T(4,128)} %copy.111.refs_1_.refs_0_, bf16[2,2304,5760]{2,1,0:T(8,128)(2,1)} %refs_2_.5, ...), custom_call_target="tpu_custom_call" | custom-call | tf_op jit(solution)/shard_map/pallas_call | solution.py:157
  725.1 23.4 %shard_map.68.refs_3_ = bf16[1024,2304]{1,0:T(8,128)(2,1)} custom-call(s32[21]{0:T(128)} %pad_add_fusion.6.blk, s32[1]{0:T(128)} %bitcast.10.scal, s32[2048,1]{1,0:T(8,128)} %copy.112.pos_ref, f32[2048,2]{1,0:T(8,128)} %pad_maximum_fusion.1.gate_ref, bf16[1024,2304]{1,0:T(8,128)(2,1)} %get-tuple-element.23.hot_ref, ...), custom_call_target="tpu_custom_call" | custom-call | tf_op jit(solution)/shard_map/pallas_call | solution.py:218
  751.6 1.3 select_select_fusion
  752.9 1.3 pad_maximum_fusion.gate_ref
  754.2 78.6 %shard_map.69 = (bf16[2048,2304]{1,0:T(8,128)(2,1)}, bf16[1024,5760]{1,0:T(8,128)(2,1)}) custom-call(bf16[2048,2304]{1,0:T(8,128)(2,1)} %x_ref.5, s32[4,1]{1,0:T(4,128)} %copy.113.refs_0_, bf16[1,2304,5760]{2,1,0:T(8,128)(2,1)} %collective-permute-done.refs_3_.refs_1_.refs_4_, ...), custom_call_target="tpu_custom_call", output_to_operand_aliasing={{0}: (5, {})} | custom-call | tf_op jit(solution)/shard_map/pallas_call | solution.py:157
  832.9 40.7 %shard_map.70.part_ref = f32[2048,2304]{1,0:T(8,128)} custom-call(s32[21]{0:T(128)} %pad_add_fusion.5.blk, s32[1]{0:T(128)} %bitcast.10.scal, s32[2048,1]{1,0:T(8,128)} %copy-done, f32[2048,2]{1,0:T(8,128)} %pad_maximum_fusion.gate_ref, bf16[2048,2304]{1,0:T(8,128)(2,1)} %get-tuple-element.24.hot_ref, bf16[16384,2304]{1,0:T(8,128)(2,1)} %get-tuple-element.22.cold_ref), custom_call_target="tpu_custom_call" | custom-call | tf_op jit(solution)/shard_map/pallas_call | solution.py:218
  873.6 7.7 shard_map.71.prev_ref
  881.3 7.7 shard_map.72
  (72 shorter events, 16.7 us)
Async XLA Ops:
  31.5 231.0 %collective-permute-start = (bf16[1,2304,5760]{2,1,0:T(8,128)(2,1)}, bf16[1,2304,5760]{2,1,0:T(8,128)(2,1)}, u32[]{:S(2)}, u32[]{:S(2)}) collective-permute-start(bf16[1,2304,5760]{2,1,0:T(8,128)(2,1)} %constant_dynamic-slice_fusion.3.dep), channel_id=1, source_target_pairs={{0,1},{1,0},{2,3},{3,2},{4,5},{5,4},{6,7},{7,6}} | collective-permute-start | bytes 79626248 | tf_op jit(solution)/shard_map/ppermute | solution.py:284
  53.0 209.5 %collective-permute-start.1 = (bf16[1,5760,2304]{2,1,0:T(8,128)(2,1)}, bf16[1,5760,2304]{2,1,0:T(8,128)(2,1)}, u32[]{:S(2)}, u32[]{:S(2)}) collective-permute-start(bf16[1,5760,2304]{2,1,0:T(8,128)(2,1)} %constant_dynamic-slice_fusion.2.dep), channel_id=1, source_target_pairs={{0,1},{1,0},{2,3},{3,2},{4,5},{5,4},{6,7},{7,6}} | collective-permute-start | bytes 79626248 | tf_op jit(solution)/shard_map/ppermute | solution.py:284
  77.5 18.9 %copy-start.1 = (s32[2048,2]{0,1:T(2,128)S(1)}, s32[2048,2]{0,1:T(2,128)}, u32[]{:S(2)}) copy-start(s32[2048,2]{0,1:T(2,128)} %param.6) | copy-start | bytes 49156
  77.5 22.7 %copy-start.3 = (f32[2048,2]{0,1:T(2,128)S(1)}, f32[2048,2]{0,1:T(2,128)}, u32[]{:S(2)}) copy-start(f32[2048,2]{0,1:T(2,128)} %param.7) | copy-start | bytes 49156
  77.5 360.8 %collective-permute-start.6 = (bf16[1,2304,5760]{2,1,0:T(8,128)(2,1)}, bf16[1,2304,5760]{2,1,0:T(8,128)(2,1)}, u32[]{:S(2)}, u32[]{:S(2)}) collective-permute-start(bf16[1,2304,5760]{2,1,0:T(8,128)(2,1)} %constant_dynamic-slice_fusion.1), channel_id=1, source_target_pairs={{0,1},{1,0},{2,3},{3,2},{4,5},{5,4},{6,7},{7,6}} | collective-permute-start | bytes 79626248 | tf_op jit(solution)/shard_map/ppermute | solution.py:284
  95.9 342.3 %collective-permute-start.7 = (bf16[1,5760,2304]{2,1,0:T(8,128)(2,1)}, bf16[1,5760,2304]{2,1,0:T(8,128)(2,1)}, u32[]{:S(2)}, u32[]{:S(2)}) collective-permute-start(bf16[1,5760,2304]{2,1,0:T(8,128)(2,1)} %constant_dynamic-slice_fusion), channel_id=1, source_target_pairs={{0,1},{1,0},{2,3},{3,2},{4,5},{5,4},{6,7},{7,6}} | collective-permute-start | bytes 79626248 | tf_op jit(solution)/shard_map/ppermute | solution.py:284
  96.4 3.7 collective-permute-start.2
  100.2 6.5 collective-permute-start.3
  106.7 102.7 %collective-permute-start.5 = (bf16[1024,2304]{1,0:T(8,128)(2,1)S(1)}, bf16[1024,2304]{1,0:T(8,128)(2,1)}, u32[]{:S(2)}, u32[]{:S(2)}) collective-permute-start(bf16[1024,2304]{1,0:T(8,128)(2,1)S(1)} %get-tuple-element.35), channel_id=1, source_target_pairs={{0,2},{1,3},{2,0},{3,1},{4,6},{5,7},{6,4},{7,5}} | collective-permute-start | bytes 14155784 | tf_op jit(solution)/shard_map/ppermute | solution.py:284
  209.4 210.3 %collective-permute-start.4 = (bf16[1024,2304]{1,0:T(8,128)(2,1)}, bf16[1024,2304]{1,0:T(8,128)(2,1)}, u32[]{:S(2)}, u32[]{:S(2)}) collective-permute-start(bf16[1024,2304]{1,0:T(8,128)(2,1)} %get-tuple-element.36), channel_id=1, source_target_pairs={{0,2},{1,3},{2,0},{3,1},{4,6},{5,7},{6,4},{7,5}} | collective-permute-start | bytes 14155784 | tf_op jit(solution)/shard_map/ppermute | solution.py:284
  641.1 232.4 %collective-permute-start.9 = (bf16[1024,2304]{1,0:T(8,128)(2,1)}, bf16[1024,2304]{1,0:T(8,128)(2,1)}, u32[]{:S(2)}, u32[]{:S(2)}) collective-permute-start(bf16[1024,2304]{1,0:T(8,128)(2,1)} %shard_map.66.refs_6_), channel_id=1, source_target_pairs={{0,2},{1,3},{2,0},{3,1},{4,6},{5,7},{6,4},{7,5}} | collective-permute-start | bytes 14155784 | tf_op jit(solution)/shard_map/ppermute | solution.py:284
  725.0 23.5 %copy-start.5 = (s32[4,1]{0,1:T(1,128)S(1)}, s32[4,1]{0,1:T(1,128)}, u32[]{:S(2)}) copy-start(s32[4,1]{0,1:T(1,128)} %get-tuple-element.54) | copy-start | bytes 52
  725.0 25.3 %copy-start.2 = (s32[2048,2]{0,1:T(2,128)S(1)}, s32[2048,2]{0,1:T(2,128)}, u32[]{:S(2)}) copy-start(s32[2048,2]{0,1:T(2,128)} %param.6) | copy-start | bytes 49156
  725.0 25.8 %copy-start.4 = (f32[2048,2]{0,1:T(2,128)S(1)}, f32[2048,2]{0,1:T(2,128)}, u32[]{:S(2)}) copy-start(f32[2048,2]{0,1:T(2,128)} %param.7) | copy-start | bytes 49156
  748.5 132.8 %collective-permute-start.8 = (bf16[1024,2304]{1,0:T(8,128)(2,1)}, bf16[1024,2304]{1,0:T(8,128)(2,1)}, u32[]{:S(2)}, u32[]{:S(2)}) collective-permute-start(bf16[1024,2304]{1,0:T(8,128)(2,1)} %shard_map.68.refs_3_), channel_id=1, source_target_pairs={{0,2},{1,3},{2,0},{3,1},{4,6},{5,7},{6,4},{7,5}} | collective-permute-start | bytes 14155784 | tf_op jit(solution)/shard_map/ppermute | solution.py:284
  750.3 82.5 %copy-start = (s32[2048,1]{1,0:T(8,128)}, s32[2048,1]{1,0:T(8,128)S(1)}, u32[]{:S(2)}) copy-start(s32[2048,1]{1,0:T(8,128)S(1)} %copy.114.pos_ref) | copy-start | bytes 24580
